TPU v7x, 32 devices: a whole 2x2x4 slice. The times are simulated.
32 devices in a mesh: dp: 4 (over y, core), tensor: 8 (over z, x).
Axes of the slice: x: 2, y: 2, z: 4, core: 2. Of those that a mesh axis runs over, the one named last changes fastest.
Arguments:
- query_latent: bfloat16 [64, 1536], P(('dp', 'tensor')), may hold values from -40 to 40
- key_value_latent: bfloat16 [64, 512], P(('dp', 'tensor')), may hold values from -40 to 40
- query_gain: float32 [1536], replicated, may hold values from 0.5 to 1.5
- key_value_gain: float32 [512], replicated, may hold values from 0.5 to 1.5
- q_up: bfloat16 [1536, 3072], P(None, 'tensor'), may hold values from -0.625 to 0.625
- kv_up: bfloat16 [512, 4096], P(None, 'tensor'), may hold values from -1 to 1
- grad_q: bfloat16 [64, 3072], P('dp', 'tensor'), may hold values from -0.23925781 to 0.23925781
- grad_kv: bfloat16 [64, 4096], P('dp', 'tensor'), may hold values from -0.23925781 to 0.23925781
Outputs:
- query_latent_gradient: float32 [64, 1536], P(('dp', 'tensor'))
- key_value_latent_gradient: float32 [64, 512], P(('dp', 'tensor'))
- d_q_up: float32 [1536, 3072], P('dp', 'tensor')
- d_kv_up: float32 [512, 4096], P('dp', 'tensor')
All inputs are finite; a program needn't handle non-finite values.
Results may differ from a plain program's by a relative error of at most 0.0029.
Values may be sent and summed in bfloat16 or wider, within the bound.
No kernel may reach another device: no remote copies, remote signals or barrier semaphores. Data moves between devices by JAX's collectives and lax.ppermute only.
A program may use at most 64 MiB of HBM per device.

v0:
```python
import jax
import jax.numpy as jnp
from jax import lax
from jax.sharding import PartitionSpec as P

EPS = 1e-06


def apply_norm(raw, norm_gain):
    input_values = raw.astype(jnp.float32)
    inverse_norm = lax.rsqrt(jnp.mean(input_values * input_values, axis=-1, keepdims=True) + EPS)
    unit_input = input_values * inverse_norm
    return (unit_input, inverse_norm, (norm_gain * unit_input).astype(jnp.bfloat16))


def backward_of_norm(incoming_gradient, unit_input, inverse_norm, norm_gain):
    scaled_gradient = norm_gain * incoming_gradient
    mean_correction = jnp.mean(scaled_gradient * unit_input, axis=-1, keepdims=True)
    return inverse_norm * (scaled_gradient - unit_input * mean_correction)


def contract_rows(left, right):
    return lax.dot_general(
        left, right, (((0,), (0,)), ((), ())), preferred_element_type=jnp.float32
    )


def contract_cols(left, right):
    return lax.dot_general(
        left, right, (((1,), (1,)), ((), ())), preferred_element_type=jnp.float32
    )


def body(query_latent, key_value_latent, query_gain, key_value_gain, q_up, kv_up, grad_q, grad_kv):
    query_width = query_latent.shape[1]
    whole_q, whole_kv = (
        lax.all_gather(query_latent, "tensor", axis=0, tiled=True),
        lax.all_gather(key_value_latent, "tensor", axis=0, tiled=True),
    )
    part_q = contract_rows(apply_norm(whole_q, query_gain)[2], grad_q)
    part_kv = contract_rows(apply_norm(whole_kv, key_value_gain)[2], grad_kv)
    d_q_up, d_kv_up = (
        lax.psum_scatter(part_q, "dp", scatter_dimension=0, tiled=True),
        lax.psum_scatter(part_kv, "dp", scatter_dimension=0, tiled=True),
    )
    summed_products = lax.psum_scatter(
        jnp.concatenate((contract_cols(grad_q, q_up), contract_cols(grad_kv, kv_up)), axis=1),
        "tensor",
        scatter_dimension=0,
        tiled=True,
    )
    query_unit, query_inverse_norm, unused_item = apply_norm(query_latent, query_gain)
    key_value_unit, key_value_inverse_norm, unused_item = apply_norm(
        key_value_latent, key_value_gain
    )
    query_latent_gradient = backward_of_norm(
        summed_products[:, :query_width], query_unit, query_inverse_norm, query_gain
    )
    key_value_latent_gradient = backward_of_norm(
        summed_products[:, query_width:], key_value_unit, key_value_inverse_norm, key_value_gain
    )
    return (query_latent_gradient, key_value_latent_gradient, d_q_up, d_kv_up)


def solution(mesh):
    return jax.shard_map(
        body,
        mesh=mesh,
        in_specs=(
            P(("dp", "tensor"), None),
            P(("dp", "tensor"), None),
            P(),
            P(),
            P(None, "tensor"),
            P(None, "tensor"),
            P("dp", "tensor"),
            P("dp", "tensor"),
        ),
        out_specs=(
            P(("dp", "tensor"), None),
            P(("dp", "tensor"), None),
            P("dp", "tensor"),
            P("dp", "tensor"),
        ),
        check_vma=False,
    )
```

profile of v0, /device:TPU:0, one launch (start us, length us, event | category | flops | bytes accessed | tf_op | source)
XLA Modules:
  0.0 113.6 jit_solution(14444127462413539571)
XLA Ops:
  8.0 0.0 copy-start
  8.1 0.0 all-reduce.3.cloned.1.call-start
  8.1 1.2 %copy-done = bf16[1536,384]{1,0:T(8,128)(2,1)S(1)} copy-done((bf16[1536,384]{1,0:T(8,128)(2,1)S(1)}, bf16[1536,384]{1,0:T(8,128)(2,1)}, u32[]{:S(2)}) %copy-start) | copy-done | bytes 1179672
  9.3 1.1 fusion.18
  10.4 0.0 copy-done.4
  10.4 0.3 fusion.19
  10.6 0.7 pad_maximum_fusion
  11.3 0.0 all-reduce.3.cloned.1.call-update
  11.3 0.0 reduce-scatter.5.cloned.1.call-start
  11.4 27.9 %all-gather.1 = bf16[8,2,512]{2,1,0:T(2,128)(2,1)S(1)} all-gather(bf16[1,2,512]{2,1,0:T(2,128)(2,1)S(1)} %bitcast.10), channel_id=1, replica_groups=mesh['dp'=4,'tensor'=8] {'tensor'}, dimensions={0}, use_global_device_ids=true | all-gather | bytes 18432 | tf_op jit(solution)/shard_map/all_gather | solution.py:38
  39.3 0.1 multiply_reduce_fusion.1
  39.5 0.0 copy-done.7
  39.5 0.0 copy-start.3
  39.5 0.0 copy-start.5
  39.5 1.4 %fusion.3 = f32[512,512]{1,0:T(8,128)} fusion(bf16[16,512]{1,0:T(8,128)(2,1)S(1)} %copy-done.4, f32[16,512]{1,0:T(8,128)S(1)} %reshape.55, f32[16]{0:T(128)S(1)} %add_rsqrt_fusion, f32[512]{0:T(512)S(1)} %copy-done.7), kind=kOutput, calls=%fused_computation.8 | convolution fusion | flops 8413184 | bytes 1099840 | tf_op jit(solution)/shard_map/dot_general | solution.py:23
  40.9 0.0 reduce-scatter.5.cloned.1.call-update
  40.9 0.0 reduce-scatter.3.cloned.1.call-start
  41.0 30.8 %all-gather = bf16[8,2,1536]{2,1,0:T(2,128)(2,1)S(1)} all-gather(bf16[1,2,1536]{2,1,0:T(2,128)(2,1)S(1)} %bitcast.9), channel_id=1, replica_groups=mesh['dp'=4,'tensor'=8] {'tensor'}, dimensions={0}, use_global_device_ids=true | all-gather | bytes 55296 | tf_op jit(solution)/shard_map/all_gather | solution.py:37
  71.8 0.1 multiply_reduce_fusion
  71.9 0.0 copy-done.5
  71.9 2.0 %fusion = f32[1536,384]{1,0:T(8,128)} fusion(bf16[16,384]{1,0:T(8,128)(2,1)S(1)} %copy-done.5, f32[16,1536]{1,0:T(8,128)S(1)} %reshape.54, f32[16]{0:T(128)S(1)} %add_rsqrt_fusion.1, f32[1536]{0:T(1024)S(1)} %copy-done.3), kind=kOutput, calls=%fused_computation.3 | convolution fusion | flops 18948096 | bytes 2476096 | tf_op jit(solution)/shard_map/dot_general | solution.py:23
  73.9 0.0 reduce-scatter.3.cloned.1.call-update
  73.9 0.6 copy-done.8
  74.6 0.6 dynamic-slice
  75.8 0.1 fusion.17
  75.9 0.1 fusion.11
  76.1 9.4 %all-reduce.3.cloned.1.call-done = f32[16,2048]{1,0:T(8,128)} async-done(((f32[16,2048]{1,0:T(8,128)}), f32[16,2048]{1,0:T(8,128)}) %all-reduce.3.cloned.1.call-update) | async-done | bytes 131088
  85.5 0.9 fusion.14
  86.4 1.0 fusion.8
  87.4 1.4 %fusion.16 = f32[2,512]{1,0:T(2,128)} fusion(bf16[2,512]{1,0:T(2,128)(2,1)S(1)} %copy-done.6, f32[2]{0:T(128)S(1)} %broadcast_multiply_fusion, f32[2]{0:T(128)S(1)} %add_rsqrt_fusion.2, f32[16,2048]{1,0:T(8,128)} %all-reduce.3.cloned.1.call-done, u32[]{:T(128)S(6)} %multiply.37, u32[]{:T(128)S(6)} %convert, f32[512]{0:T(512)S(1)} %copy-done.7), kind=kLoop, calls=%fused_computation.26 | loop fusion | flops 6144 | bytes 12312 | tf_op jit(solution)/shard_map/mul | solution.py:19
  88.8 1.5 %fusion.10 = f32[2,1536]{1,0:T(2,128)} fusion(bf16[2,1536]{1,0:T(2,128)(2,1)S(1)} %copy-done.2, f32[16,2048]{1,0:T(8,128)} %all-reduce.3.cloned.1.call-done, u32[]{:T(128)S(6)} %multiply.37, f32[2]{0:T(128)S(1)} %broadcast_multiply_fusion.1, f32[2]{0:T(128)S(1)} %add_rsqrt_fusion.3, f32[1536]{0:T(1024)S(1)} %copy-done.3), kind=kLoop, calls=%fused_computation.17 | loop fusion | flops 18432 | bytes 36884 | tf_op jit(solution)/shard_map/mul | solution.py:19
  90.3 15.9 %reduce-scatter.3.cloned.1.call-done = f32[384,384]{1,0:T(8,128)} async-done(((f32[1536,384]{1,0:T(8,128)}), f32[384,384]{1,0:T(8,128)}) %reduce-scatter.3.cloned.1.call-update) | async-done | bytes 589840 | tf_op jit(solution)/shard_map/reduce_scatter | solution.py:43
  (19 shorter events, 0.1 us)
Async XLA Ops:
  8.0 1.3 %copy-start = (bf16[1536,384]{1,0:T(8,128)(2,1)S(1)}, bf16[1536,384]{1,0:T(8,128)(2,1)}, u32[]{:S(2)}) copy-start(bf16[1536,384]{1,0:T(8,128)(2,1)} %param.12) | copy-start | bytes 3538948
  8.0 2.4 %copy-start.1 = (bf16[512,512]{1,0:T(8,128)(2,1)S(1)}, bf16[512,512]{1,0:T(8,128)(2,1)}, u32[]{:S(2)}) copy-start(bf16[512,512]{1,0:T(8,128)(2,1)} %param.13) | copy-start | bytes 1572868
  8.0 2.4 %copy-start.4 = (bf16[16,512]{1,0:T(8,128)(2,1)S(1)}, bf16[16,512]{1,0:T(8,128)(2,1)}, u32[]{:S(2)}) copy-start(bf16[16,512]{1,0:T(8,128)(2,1)} %param.15) | copy-start | bytes 49156
  8.0 3.4 %copy-start.6 = (bf16[2,512]{1,0:T(2,128)(2,1)S(1)}, bf16[2,512]{1,0:T(2,128)(2,1)}, u32[]{:S(2)}) copy-start(bf16[2,512]{1,0:T(2,128)(2,1)} %param.9) | copy-start | bytes 6148
  8.0 31.4 %copy-start.7 = (f32[512]{0:T(512)S(1)}, f32[512]{0:T(512)}, u32[]{:S(2)}) copy-start(f32[512]{0:T(512)} %param.11) | copy-start | bytes 6148
  8.1 77.4 %all-reduce.3.cloned.1.call-start = ((), (), s32[]{:S(2)}) async-start(), calls=%async_computation.4 | async-start | bytes 262144
  11.3 29.6 %copy-start.2 = (bf16[2,1536]{1,0:T(2,128)(2,1)S(1)}, bf16[2,1536]{1,0:T(2,128)(2,1)}, u32[]{:S(2)}) copy-start(bf16[2,1536]{1,0:T(2,128)(2,1)} %param.8) | copy-start | bytes 18436
  11.3 78.9 %reduce-scatter.5.cloned.1.call-start = ((), (), s32[]{:S(2)}) async-start(), calls=%async_computation.3 | async-start | bytes 1310720 | tf_op jit(solution)/shard_map/reduce_scatter | solution.py:44
  39.5 32.4 %copy-start.3 = (f32[1536]{0:T(1024)S(1)}, f32[1536]{0:T(1024)}, u32[]{:S(2)}) copy-start(f32[1536]{0:T(1024)} %param.10) | copy-start | bytes 18436
  39.5 32.4 %copy-start.5 = (bf16[16,384]{1,0:T(8,128)(2,1)S(1)}, bf16[16,384]{1,0:T(8,128)(2,1)}, u32[]{:S(2)}) copy-start(bf16[16,384]{1,0:T(8,128)(2,1)} %param.14) | copy-start | bytes 36868
  40.9 65.2 %reduce-scatter.3.cloned.1.call-start = ((), (), s32[]{:S(2)}) async-start(), calls=%async_computation.2 | async-start | bytes 2949120 | tf_op jit(solution)/shard_map/reduce_scatter | solution.py:43
  73.9 0.7 copy-start.8
Sparse Core Ops, SparseCore 0:
  12.2 73.2 all-reduce.2
Sparse Core Ops, SparseCore 1:
  41.0 24.1 reduce-scatter.4
  74.0 32.0 reduce-scatter.2
where the time goes:
time: 114 us
  blocking collectives  58.7 us (51%)
  waiting for transfers between devices  25.3 us (22%)
  between operations  16.3 us (14%)
  other arithmetic  5.96 us (5%)
  matrix products  4.73 us (4%)
  local copies, waits for them, and re-layouts  2.45 us (2%)
    all_gather x1, blocking collectives, body(): lax.all_gather(query_latent, 'tensor', axis=0, tiled=True)  30.8 us
    all_gather x1, blocking collectives, body(): lax.all_gather(key_value_latent, 'tensor', axis=0, tiled=True)  27.9 us
    reduce_scatter x1, waiting for transfers between devices, body(): lax.psum_scatter(part_q, 'dp', scatter_dimension=0, tiled=True)  15.9 us
    unnamed x4, waiting for transfers between devices  9.45 us
    dot_general x2, matrix products, contract_rows(): lax.dot_general(left, right, (((0,), (0,)), ((), ())), preferred_element_...  3.37 us
    mul x2, other arithmetic, backward_of_norm(): return inverse_norm * (scaled_gradient - unit_input * mean_correction)  2.87 us
    unnamed x19, local copies, waits for them, and re-layouts  2.42 us
  transfers between devices with their start and end apart: 3, of which 2 were waited for; matrix products, arithmetic and copies ran while one was open for 8% of the time, Pallas kernels for 0%

commit v1 on v0

--- a/solution.py
+++ b/solution.py
@@ -34,7 +34,15 @@
 def body(query_latent, key_value_latent, query_gain, key_value_gain, q_up, kv_up, grad_q, grad_kv):
     query_width = query_latent.shape[1]
     whole_q, whole_kv = (
-        lax.all_gather(query_latent, "tensor", axis=0, tiled=True),
+        jnp.concatenate(
+            lax.all_to_all(
+                jnp.stack([query_latent for _ in range(lax.axis_size("tensor"))], axis=0),
+                "tensor",
+                0,
+                0,
+            ),
+            0,
+        ),
         lax.all_gather(key_value_latent, "tensor", axis=0, tiled=True),
     )
     part_q = contract_rows(apply_norm(whole_q, query_gain)[2], grad_q)

time: 114 us -> 109 us (0.956)
  blocking collectives: 58.7 us -> 38.5 us
  waiting for transfers between devices: 25.3 us -> 40.2 us
    all_gather x1 -> x0, blocking collectives: 30.8 us -> none  [body(): lax.all_gather(query_latent, 'tensor', axis=0, tiled=True)]
    unnamed x4, waiting for transfers between devices: 9.45 us -> 29.5 us
    all_to_all x0 -> x1, blocking collectives: none -> 10.6 us  [body(): lax.all_to_all(jnp.stack([query_latent for _ in range(lax.axis_size('tens...]
    reduce_scatter x1, waiting for transfers between devices: 15.9 us -> 10.7 us  [body(): lax.psum_scatter(part_q, 'dp', scatter_dimension=0, tiled=True)]
  transfers between devices with their start and end apart: 3 -> 3, of which waited for: 2 -> 2; matrix products, arithmetic and copies ran while one was open for 8% -> 9% of each run, Pallas kernels for 0% -> 0%
where the time goes in v1:
time: 109 us; the launch traced here: 108 us
  waiting for transfers between devices  40.2 us (37%)
  blocking collectives  38.5 us (35%)
  between operations  16.3 us (15%)
  other arithmetic  5.97 us (5%)
  matrix products  4.73 us (4%)
  local copies, waits for them, and re-layouts  2.56 us (2%)
    unnamed x4, waiting for transfers between devices  29.5 us
    all_gather x1, blocking collectives, body(): lax.all_gather(key_value_latent, 'tensor', axis=0, tiled=True)  27.9 us
    reduce_scatter x1, waiting for transfers between devices, body(): lax.psum_scatter(part_q, 'dp', scatter_dimension=0, tiled=True)  10.7 us
    all_to_all x1, blocking collectives, body(): lax.all_to_all(jnp.stack([query_latent for _ in range(lax.axis_size('tens...  10.6 us
    dot_general x2, matrix products, contract_rows(): lax.dot_general(left, right, (((0,), (0,)), ((), ())), preferred_element_...  3.37 us
    mul x2, other arithmetic, backward_of_norm(): return inverse_norm * (scaled_gradient - unit_input * mean_correction)  2.87 us
    unnamed x19, local copies, waits for them, and re-layouts  2.43 us
  transfers between devices with their start and end apart: 3, of which 2 were waited for; matrix products, arithmetic and copies ran while one was open for 9% of the time, Pallas kernels for 0%

profile of v1, /device:TPU:0, one launch (start us, length us, event | category | flops | bytes accessed | tf_op | source)
XLA Modules:
  0.0 108.4 jit_solution(14065719198789259860)
XLA Ops:
  8.0 0.0 copy-start
  8.1 0.0 all-reduce.3.cloned.1.call-start
  8.1 1.2 %copy-done = bf16[1536,384]{1,0:T(8,128)(2,1)S(1)} copy-done((bf16[1536,384]{1,0:T(8,128)(2,1)S(1)}, bf16[1536,384]{1,0:T(8,128)(2,1)}, u32[]{:S(2)}) %copy-start) | copy-done | bytes 1179672
  9.3 1.1 %fusion.18 = f32[16,1536]{1,0:T(8,128)S(1)} fusion(bf16[16,384]{1,0:T(8,128)(2,1)} %param.14, bf16[1536,384]{1,0:T(8,128)(2,1)S(1)} %copy-done), kind=kOutput, calls=%fused_computation.35 | convolution fusion | flops 18874368 | bytes 1290240 | tf_op jit(solution)/shard_map/dot_general | solution.py:29
  10.4 0.0 copy-done.4
  10.4 0.3 fusion.19
  10.6 0.7 pad_maximum_fusion
  11.3 0.0 all-reduce.3.cloned.1.call-update
  11.3 0.0 reduce-scatter.5.cloned.1.call-start
  11.4 27.9 %all-gather = bf16[8,2,512]{2,1,0:T(2,128)(2,1)S(1)} all-gather(bf16[1,2,512]{2,1,0:T(2,128)(2,1)S(1)} %bitcast.8), channel_id=1, replica_groups=mesh['dp'=4,'tensor'=8] {'tensor'}, dimensions={0}, use_global_device_ids=true | all-gather | bytes 18432 | tf_op jit(solution)/shard_map/all_gather | solution.py:46
  39.3 0.1 multiply_reduce_fusion.1
  39.5 0.0 copy-done.7
  39.5 0.0 copy-start.3
  39.5 0.0 copy-start.5
  39.5 1.4 %fusion.3 = f32[512,512]{1,0:T(8,128)} fusion(bf16[16,512]{1,0:T(8,128)(2,1)S(1)} %copy-done.4, f32[16,512]{1,0:T(8,128)S(1)} %reshape.67, f32[16]{0:T(128)S(1)} %add_rsqrt_fusion.1, f32[512]{0:T(512)S(1)} %copy-done.7), kind=kOutput, calls=%fused_computation.8 | convolution fusion | flops 8413184 | bytes 1099840 | tf_op jit(solution)/shard_map/dot_general | solution.py:23
  40.9 0.0 reduce-scatter.5.cloned.1.call-update
  40.9 0.0 reduce-scatter.3.cloned.1.call-start
  41.0 10.6 %all_to_all.5 = bf16[8,2,1536]{2,1,0:T(2,128)(2,1)S(1)} all-to-all(bf16[8,2,1536]{2,1,0:T(2,128)(2,1)S(1)} %stack.2), channel_id=1, replica_groups=mesh['dp'=4,'tensor'=8] {'tensor'}, dimensions={0} | all-to-all | bytes 98304 | tf_op jit(solution)/shard_map/all_to_all | solution.py:38
  51.6 0.1 multiply_reduce_fusion
  51.7 0.1 rsqrt.38
  51.8 2.0 %fusion = f32[1536,384]{1,0:T(8,128)} fusion(bf16[16,384]{1,0:T(8,128)(2,1)S(1)} %copy-done.5, f32[16,1536]{1,0:T(8,128)S(1)} %reshape.64, f32[16]{0:T(128)S(1)} %rsqrt.38, f32[1536]{0:T(1024)S(1)} %copy-done.3), kind=kOutput, calls=%fused_computation.3 | convolution fusion | flops 18948096 | bytes 2476096 | tf_op jit(solution)/shard_map/dot_general | solution.py:23
  53.8 0.0 reduce-scatter.3.cloned.1.call-update
  53.9 0.6 copy-done.8
  54.5 0.6 dynamic-slice
  55.7 0.1 fusion.17
  55.8 0.1 fusion.11
  56.0 29.5 %all-reduce.3.cloned.1.call-done = f32[16,2048]{1,0:T(8,128)} async-done(((f32[16,2048]{1,0:T(8,128)}), f32[16,2048]{1,0:T(8,128)}) %all-reduce.3.cloned.1.call-update) | async-done | bytes 131088
  85.5 0.9 fusion.14
  86.4 1.0 fusion.8
  87.4 1.4 %fusion.16 = f32[2,512]{1,0:T(2,128)} fusion(bf16[2,512]{1,0:T(2,128)(2,1)S(1)} %copy-done.6, f32[2]{0:T(128)S(1)} %broadcast_multiply_fusion, f32[2]{0:T(128)S(1)} %add_rsqrt_fusion.2, f32[16,2048]{1,0:T(8,128)} %all-reduce.3.cloned.1.call-done, u32[]{:T(128)S(6)} %multiply.38, u32[]{:T(128)S(6)} %convert.1, f32[512]{0:T(512)S(1)} %copy-done.7), kind=kLoop, calls=%fused_computation.26 | loop fusion | flops 6144 | bytes 12312 | tf_op jit(solution)/shard_map/mul | solution.py:19
  88.8 1.5 %fusion.10 = f32[2,1536]{1,0:T(2,128)} fusion(bf16[2,1536]{1,0:T(2,128)(2,1)S(1)} %copy-done.2, f32[16,2048]{1,0:T(8,128)} %all-reduce.3.cloned.1.call-done, u32[]{:T(128)S(6)} %multiply.38, f32[2]{0:T(128)S(1)} %broadcast_multiply_fusion.1, f32[2]{0:T(128)S(1)} %add_rsqrt_fusion.3, f32[1536]{0:T(1024)S(1)} %copy-done.3), kind=kLoop, calls=%fused_computation.17 | loop fusion | flops 18432 | bytes 36884 | tf_op jit(solution)/shard_map/mul | solution.py:19
  90.3 10.7 %reduce-scatter.3.cloned.1.call-done = f32[384,384]{1,0:T(8,128)} async-done(((f32[1536,384]{1,0:T(8,128)}), f32[384,384]{1,0:T(8,128)}) %reduce-scatter.3.cloned.1.call-update) | async-done | bytes 589840 | tf_op jit(solution)/shard_map/reduce_scatter | solution.py:51
  (21 shorter events, 0.1 us)
Async XLA Ops:
  8.0 1.3 %copy-start = (bf16[1536,384]{1,0:T(8,128)(2,1)S(1)}, bf16[1536,384]{1,0:T(8,128)(2,1)}, u32[]{:S(2)}) copy-start(bf16[1536,384]{1,0:T(8,128)(2,1)} %param.12) | copy-start | bytes 3538948
  8.0 2.4 %copy-start.1 = (bf16[512,512]{1,0:T(8,128)(2,1)S(1)}, bf16[512,512]{1,0:T(8,128)(2,1)}, u32[]{:S(2)}) copy-start(bf16[512,512]{1,0:T(8,128)(2,1)} %param.13) | copy-start | bytes 1572868
  8.0 2.4 %copy-start.4 = (bf16[16,512]{1,0:T(8,128)(2,1)S(1)}, bf16[16,512]{1,0:T(8,128)(2,1)}, u32[]{:S(2)}) copy-start(bf16[16,512]{1,0:T(8,128)(2,1)} %param.15) | copy-start | bytes 49156
  8.0 3.4 %copy-start.6 = (bf16[2,512]{1,0:T(2,128)(2,1)S(1)}, bf16[2,512]{1,0:T(2,128)(2,1)}, u32[]{:S(2)}) copy-start(bf16[2,512]{1,0:T(2,128)(2,1)} %param.9) | copy-start | bytes 6148
  8.0 31.4 %copy-start.7 = (f32[512]{0:T(512)S(1)}, f32[512]{0:T(512)}, u32[]{:S(2)}) copy-start(f32[512]{0:T(512)} %param.11) | copy-start | bytes 6148
  8.1 77.4 %all-reduce.3.cloned.1.call-start = ((), (), s32[]{:S(2)}) async-start(), calls=%async_computation.5 | async-start | bytes 262144
  11.3 29.6 %copy-start.2 = (bf16[2,1536]{1,0:T(2,128)(2,1)S(1)}, bf16[2,1536]{1,0:T(2,128)(2,1)}, u32[]{:S(2)}) copy-start(bf16[2,1536]{1,0:T(2,128)(2,1)} %param.8) | copy-start | bytes 18436
  11.3 78.9 %reduce-scatter.5.cloned.1.call-start = ((), (), s32[]{:S(2)}) async-start(), calls=%async_computation.4 | async-start | bytes 1310720 | tf_op jit(solution)/shard_map/reduce_scatter | solution.py:52
  39.5 12.3 %copy-start.3 = (f32[1536]{0:T(1024)S(1)}, f32[1536]{0:T(1024)}, u32[]{:S(2)}) copy-start(f32[1536]{0:T(1024)} %param.10) | copy-start | bytes 18436
  39.5 12.3 %copy-start.5 = (bf16[16,384]{1,0:T(8,128)(2,1)S(1)}, bf16[16,384]{1,0:T(8,128)(2,1)}, u32[]{:S(2)}) copy-start(bf16[16,384]{1,0:T(8,128)(2,1)} %param.14) | copy-start | bytes 36868
  40.9 60.0 %reduce-scatter.3.cloned.1.call-start = ((), (), s32[]{:S(2)}) async-start(), calls=%async_computation.3 | async-start | bytes 2949120 | tf_op jit(solution)/shard_map/reduce_scatter | solution.py:51
  53.8 0.7 copy-start.8
Sparse Core Ops, SparseCore 0:
  12.2 73.2 all-reduce.2
Sparse Core Ops, SparseCore 1:
  41.0 24.1 reduce-scatter.4
  68.2 32.7 reduce-scatter.2
